TPU v7x, 32 devices: a whole 2x2x4 slice. The times are simulated.
32 devices in a mesh: groups: 2 (over y), geom: 4 (over z), design: 2 (over x), head: 2 (over core).
Axes of the slice: x: 2, y: 2, z: 4, core: 2. Of those that a mesh axis runs over, the one named last changes fastest.
Arguments:
- point_feats: bfloat16 [4, 12288, 192], P(('groups', 'design'), ('geom', 'head')), parts along dimension 0, may hold values from -6 to 6
- block_anchor: int32 [4, 96], P(('groups', 'design'), ('geom', 'head')), parts along dimension 0, may hold values from 0 to 127, as said below
- anchor_feats: bfloat16 [4, 128, 192], P(('groups', 'design'), ('geom', 'head')), parts along dimension 0, may hold values from -4 to 4
- query_feats: bfloat16 [4, 4096, 192], P(('groups', 'design'), ('geom', 'head')), parts along dimension 0, may hold values from -6 to 6
- out_grad: bfloat16 [4, 4096, 192], P(('groups', 'design'), ('geom', 'head')), parts along dimension 0, may hold values from -6 to 6
- norm_gain: float32 [192], replicated, may hold values from 0.5 to 1.5
- w_in: bfloat16 [192, 384], replicated, may hold values from -0.4375 to 0.4375
- w_out: bfloat16 [384, 192], replicated, may hold values from -0.3125 to 0.3125
- w_query: bfloat16 [192, 192], replicated, may hold values from -0.4375 to 0.4375
- w_key: bfloat16 [192, 192], replicated, may hold values from -0.4375 to 0.4375
- w_value: bfloat16 [192, 192], replicated, may hold values from -0.4375 to 0.4375
- w_proj: bfloat16 [192, 192], replicated, may hold values from -0.4375 to 0.4375
Outputs:
- attended: bfloat16 [4, 4096, 192], P(('groups', 'design'), ('geom', 'head')), parts along dimension 0
- point_grad: bfloat16 [4, 12288, 192], P(('groups', 'design'), ('geom', 'head')), parts along dimension 0
- grad_in: float32 [384, 384], P('groups'), parts along dimension 0
- grad_out: float32 [768, 192], P('groups'), parts along dimension 0
- grad_query: float32 [384, 192], P('groups'), parts along dimension 0
- grad_key: float32 [384, 192], P('groups'), parts along dimension 0
- grad_value: float32 [384, 192], P('groups'), parts along dimension 0
- grad_proj: float32 [384, 192], P('groups'), parts along dimension 0
- grad_gain: float32 [384], P('groups'), parts along dimension 0
There are 2 independent parts, one for each index of `groups`. A program takes and returns all parts, laid end to end along the dimension named above; an argument that names none is the same for every part. Nothing has to cross between parts.
Inputs may be any that keep to these rules, and one draw needn't show every extreme that they name: `block_anchor`: block index // 12 is the device that holds the block. Each device assigns at most 2 of its blocks to anchors of any one owner (anchor // 16); in every design one owner gets exactly 2 blocks from every device.
All inputs are finite; a program needn't handle non-finite values.
Results may differ from a plain program's by a relative error of at most 0.03.
Values may be sent and summed in bfloat16 or wider, within the bound.
No kernel may reach another device: no remote copies, remote signals or barrier semaphores. Data moves between devices by JAX's collectives and lax.ppermute only.
A program may use at most 64 MiB of HBM per device.

v0:
```python
import jax
import jax.numpy as jnp
from jax import lax
from jax.sharding import PartitionSpec as P

HEADS = 3
CAP = 2


def gelu_tanh(values):
    return jax.nn.gelu(values, approximate=True)


def contract_rows(first_arg, second_arg, precision=None):
    return lax.dot_general(
        first_arg,
        second_arg,
        (((0,), (0,)), ((), ())),
        precision=precision,
        preferred_element_type=jnp.float32,
    )


def times_transposed(first_arg, second_arg):
    return lax.dot_general(
        first_arg, second_arg, (((1,), (1,)), ((), ())), preferred_element_type=jnp.float32
    )


def head_split(matrix):
    return matrix.reshape(matrix.shape[0], HEADS, matrix.shape[1] // HEADS)


def on_device(
    point_feats,
    block_anchor,
    anchor_feats,
    query_feats,
    out_grad,
    norm_gain,
    w_in,
    w_out,
    w_query,
    w_key,
    w_value,
    w_proj,
):
    exact_mode = lax.Precision.HIGHEST
    owners = lax.axis_size(("geom", "head"))
    points = point_feats[0]
    assigned = block_anchor[0]
    anchor_rows = anchor_feats[0]
    query_rows = query_feats[0]
    cotangent = out_grad[0]
    blocks = assigned.shape[0]
    feature_width = points.shape[1]
    hidden_width = w_in.shape[1]
    anchors_here = anchor_rows.shape[0]
    block_size = points.shape[0] // blocks
    slot_count = owners * CAP
    target = assigned // anchors_here
    within = assigned - target * anchors_here
    block_order = jnp.arange(blocks)
    earlier = (target[None, :] == target[:, None]) & (block_order[None, :] < block_order[:, None])
    slot_of = target * CAP + jnp.sum(earlier.astype(jnp.int32), axis=1)
    selector = jnp.arange(slot_count)[:, None] == slot_of[None, :]
    select_bf = selector.astype(jnp.bfloat16)
    slot_anchor = jnp.sum(jnp.where(selector, within[None, :] + 1, 0), axis=1) - 1
    pre_act = jnp.dot(points, w_in, preferred_element_type=jnp.float32)
    hidden = gelu_tanh(pre_act).astype(jnp.bfloat16)
    message = jnp.dot(hidden, w_out, preferred_element_type=jnp.float32)
    block_sums = message.reshape(blocks, block_size, feature_width).sum(axis=1)
    outgoing_sums = jnp.dot(selector.astype(jnp.float32), block_sums, precision=exact_mode)
    arrived_sums, arrived_ids = (
        lax.all_to_all(
            outgoing_sums.reshape(owners, CAP, feature_width).astype(jnp.bfloat16),
            ("geom", "head"),
            split_axis=0,
            concat_axis=0,
            tiled=True,
        ).astype(jnp.float32),
        lax.all_to_all(
            slot_anchor.astype(jnp.float32).reshape(owners, CAP).astype(jnp.bfloat16),
            ("geom", "head"),
            split_axis=0,
            concat_axis=0,
            tiled=True,
        ).astype(jnp.float32),
    )
    slot_sums = arrived_sums.reshape(slot_count, feature_width)
    slot_ids = arrived_ids.reshape(slot_count).astype(jnp.int32)
    member = (jnp.arange(anchors_here)[:, None] == slot_ids[None, :]).astype(jnp.float32)
    pooled = jnp.dot(member, slot_sums, precision=exact_mode)
    divisor = jnp.maximum(jnp.sum(member, axis=1) * block_size, 1.0)
    anchor_sum = anchor_rows.astype(jnp.float32) + pooled / divisor[:, None]
    inv_rms = lax.rsqrt(jnp.mean(anchor_sum * anchor_sum, axis=1, keepdims=True) + 1e-06)
    normed = (anchor_sum * inv_rms * norm_gain).astype(jnp.bfloat16)
    key_local = jnp.dot(normed, w_key, preferred_element_type=jnp.float32).astype(jnp.bfloat16)
    value_local = jnp.dot(normed, w_value, preferred_element_type=jnp.float32).astype(jnp.bfloat16)
    all_keys, all_values = (
        lax.all_gather(key_local, ("geom", "head"), axis=0, tiled=True),
        lax.all_gather(value_local, ("geom", "head"), axis=0, tiled=True),
    )
    query_proj = jnp.dot(query_rows, w_query, preferred_element_type=jnp.float32).astype(
        jnp.bfloat16
    )
    score_scale = 1.0 / (feature_width // HEADS) ** 0.5
    query_heads = head_split(query_proj)
    key_heads = head_split(all_keys)
    value_heads = head_split(all_values)
    scores = (
        jnp.einsum("qhd,khd->hqk", query_heads, key_heads, preferred_element_type=jnp.float32)
        * score_scale
    )
    softmax_w = jax.nn.softmax(scores, axis=-1)
    softmax_bf = softmax_w.astype(jnp.bfloat16)
    mixed_heads = (
        jnp.einsum("hqk,khd->qhd", softmax_bf, value_heads, preferred_element_type=jnp.float32)
        .reshape(-1, feature_width)
        .astype(jnp.bfloat16)
    )
    attended = jnp.dot(mixed_heads, w_proj, preferred_element_type=jnp.float32).astype(jnp.bfloat16)
    grad_proj = contract_rows(mixed_heads, cotangent)
    d_mixed = times_transposed(cotangent, w_proj).astype(jnp.bfloat16)
    dmix_heads = head_split(d_mixed)
    d_probs = jnp.einsum(
        "qhd,khd->hqk", dmix_heads, value_heads, preferred_element_type=jnp.float32
    )
    d_scores = (
        softmax_w * (d_probs - jnp.sum(softmax_w * d_probs, axis=-1, keepdims=True)) * score_scale
    ).astype(jnp.bfloat16)
    d_query = (
        jnp.einsum("hqk,khd->qhd", d_scores, key_heads, preferred_element_type=jnp.float32)
        .reshape(-1, feature_width)
        .astype(jnp.bfloat16)
    )
    key_terms = jnp.einsum(
        "hqk,qhd->khd", d_scores, query_heads, preferred_element_type=jnp.float32
    ).reshape(-1, feature_width)
    value_terms = jnp.einsum(
        "hqk,qhd->khd", softmax_bf, dmix_heads, preferred_element_type=jnp.float32
    ).reshape(-1, feature_width)
    grad_query = contract_rows(query_rows, d_query)
    key_sum, value_sum = (
        lax.psum_scatter(
            key_terms.astype(jnp.bfloat16), ("geom", "head"), scatter_dimension=0, tiled=True
        ).astype(jnp.float32),
        lax.psum_scatter(
            value_terms.astype(jnp.bfloat16), ("geom", "head"), scatter_dimension=0, tiled=True
        ).astype(jnp.float32),
    )
    key_grad = key_sum.astype(jnp.bfloat16)
    value_grad = value_sum.astype(jnp.bfloat16)
    grad_key = contract_rows(normed, key_grad)
    grad_value = contract_rows(normed, value_grad)
    d_normed = times_transposed(key_grad, w_key) + times_transposed(value_grad, w_value)
    scaled = d_normed * norm_gain
    grad_gain = jnp.sum(d_normed * anchor_sum * inv_rms, axis=0)
    d_sum = inv_rms * scaled - anchor_sum * inv_rms**3 * jnp.mean(
        scaled * anchor_sum, axis=1, keepdims=True
    )
    d_pooled = d_sum / divisor[:, None]
    slot_grad = contract_rows(member, d_pooled, exact_mode).astype(jnp.bfloat16)
    returned_grad = lax.all_to_all(
        slot_grad.reshape(owners, CAP, feature_width),
        ("geom", "head"),
        split_axis=0,
        concat_axis=0,
        tiled=True,
    )
    block_grad = contract_rows(select_bf, returned_grad.reshape(slot_count, feature_width)).astype(
        jnp.bfloat16
    )
    d_hidden_block = times_transposed(block_grad, w_out)
    d_hidden = jnp.broadcast_to(
        d_hidden_block[:, None, :], (blocks, block_size, hidden_width)
    ).reshape(-1, hidden_width)
    unused_out, gelu_back = jax.vjp(gelu_tanh, pre_act)
    d_pre = gelu_back(d_hidden)[0].astype(jnp.bfloat16)
    hidden_sum = jnp.sum(
        hidden.reshape(blocks, block_size, hidden_width), axis=1, dtype=jnp.float32
    )
    grad_out = contract_rows(hidden_sum, block_grad.astype(jnp.float32), exact_mode)
    grad_in = contract_rows(points, d_pre)
    d_input = times_transposed(d_pre, w_in).astype(jnp.bfloat16)
    reduced = lax.psum(
        (grad_in, grad_out, grad_query, grad_key, grad_value, grad_proj, grad_gain),
        ("geom", "design", "head"),
    )
    return (
        attended[None],
        d_input[None],
        reduced[0],
        reduced[1],
        reduced[2],
        reduced[3],
        reduced[4],
        reduced[5],
        reduced[6],
    )


def solution(mesh):
    placed = (
        P(("groups", "design"), ("geom", "head"), None),
        P(("groups", "design"), ("geom", "head")),
        P(("groups", "design"), ("geom", "head"), None),
        P(("groups", "design"), ("geom", "head"), None),
        P(("groups", "design"), ("geom", "head"), None),
        P(),
        P(),
        P(),
        P(),
        P(),
        P(),
        P(),
    )
    return jax.shard_map(
        on_device,
        mesh=mesh,
        in_specs=placed,
        out_specs=(
            P(("groups", "design"), ("geom", "head"), None),
            P(("groups", "design"), ("geom", "head"), None),
            P("groups", None),
            P("groups", None),
            P("groups", None),
            P("groups", None),
            P("groups", None),
            P("groups", None),
            P("groups"),
        ),
        check_vma=False,
    )
```

profile of v0, /device:TPU:0, one launch (start us, length us, event | category | flops | bytes accessed | tf_op | source)
XLA Modules:
  0.0 259.6 jit_solution(16616870421361154867)
XLA Ops:
  7.2 0.7 and_select_fusion
  7.9 0.7 add_bitcast_fusion
  8.6 0.2 convert_reduce_fusion.2
  8.8 0.1 select_reduce_fusion
  8.9 0.7 convert_element_type.190
  9.6 6.4 %all-to-all-start = ((bf16[8,1,2]{2,1,0:T(2,128)(2,1)}), bf16[8,1,2]{2,1,0:T(2,128)(2,1)S(1)}, u32[]{:S(2)}, u32[]{:S(2)}) async-start(bf16[8,1,2]{2,1,0:T(2,128)(2,1)} %convert_element_type.190), calls=%async_computation | async-start | bytes 8192 | tf_op jit(solution)/shard_map/all_to_all | solution.py:82
  16.0 3.2 %multiply_convert_fusion = (bf16[1536,384]{1,0:T(8,128)(2,1)S(1)}, f32[1536,384]{1,0:T(8,128)}) fusion(bf16[192,384]{1,0:T(8,128)(2,1)} %param.18, bf16[1,1536,192]{1,2,0:T(8,128)(2,1)S(1)} %copy-done), kind=kOutput, calls=%fused_computation.19 | convolution fusion | flops 231800832 | bytes 4276224 | tf_op jit(solution)/shard_map/dot_general | solution.py:69
  19.2 0.8 convert_reduce_fusion
  20.0 0.6 fusion.64
  20.6 0.2 reshape.166
  20.8 0.1 copy-done.1
  20.9 1.2 convolution_convert_fusion.5
  22.1 1.2 convolution_convert_fusion.1
  23.3 0.5 reduce_sum.95
  23.8 0.2 convolution_convert_fusion.12
  23.9 0.7 copy.50
  24.6 5.1 %all-to-all-start.1 = ((bf16[8,2,192]{2,1,0:T(2,128)(2,1)}), bf16[8,2,192]{2,1,0:T(2,128)(2,1)S(1)}, u32[]{:S(2)}, u32[]{:S(2)}) async-start(bf16[8,2,192]{2,1,0:T(2,128)(2,1)} %copy.50), calls=%async_computation.1 | async-start | bytes 16384 | tf_op jit(solution)/shard_map/all_to_all | solution.py:75
  29.8 0.1 convert_element_type.158
  29.9 0.1 convert_reduce_fusion.1
  30.0 5.3 %all-to-all-done.1 = bf16[8,2,192]{2,1,0:T(2,128)(2,1)S(1)} async-done(((bf16[8,2,192]{2,1,0:T(2,128)(2,1)}), bf16[8,2,192]{2,1,0:T(2,128)(2,1)S(1)}, u32[]{:S(2)}, u32[]{:S(2)}) %all-to-all-start.1) | async-done | bytes 6176 | tf_op jit(solution)/shard_map/all_to_all | solution.py:75
  35.4 0.2 multiply_reduce_fusion.3
  35.6 0.1 multiply_convert_fusion.1
  35.7 0.1 convolution_convert_fusion.10
  35.8 0.1 convolution_convert_fusion.11
  36.0 14.0 %all_gather.6 = bf16[128,192]{1,0:T(8,128)(2,1)S(1)} all-gather(bf16[16,192]{1,0:T(8,128)(2,1)S(1)} %convolution_convert_fusion.11), channel_id=1, replica_groups=mesh['groups'=2,'geom'=4,'design'=2,'head'=2] {'geom','head'}, dimensions={0}, use_global_device_ids=true | all-gather | bytes 55296 | tf_op jit(solution)/shard_map/all_gather | solution.py:102
  50.0 0.1 copy.51
  50.1 14.0 %all_gather.7 = bf16[128,192]{1,0:T(8,128)(2,1)S(1)} all-gather(bf16[16,192]{1,0:T(8,128)(2,1)S(1)} %convolution_convert_fusion.10), channel_id=1, replica_groups=mesh['groups'=2,'geom'=4,'design'=2,'head'=2] {'geom','head'}, dimensions={0}, use_global_device_ids=true | all-gather | bytes 55296 | tf_op jit(solution)/shard_map/all_gather | solution.py:101
  64.1 0.1 copy.52
  64.2 0.3 fusion.65
  64.5 1.3 fusion.63
  65.8 1.8 convolution_convert_fusion.7
  67.6 1.8 convolution_convert_fusion.2
  69.4 0.6 convolution_convert_fusion.4
  70.0 0.9 convolution_bitcast_fusion.1
  70.9 0.7 copy.64
  71.7 0.0 reduce-scatter.9.cloned.1.call-start
  71.7 0.9 fusion.30
  72.6 0.6 convolution_convert_fusion.6
  73.2 0.7 copy.66
  74.0 26.5 %reduce-scatter.7.cloned.1.call-done = bf16[16,192]{1,0:T(8,128)(2,1)} async-done(((bf16[128,192]{1,0:T(8,128)(2,1)}), bf16[16,192]{1,0:T(8,128)(2,1)}) %reduce-scatter.7.cloned.1.call-update) | async-done | bytes 6160
  100.5 0.8 fusion.66
  101.4 30.6 %reduce-scatter.9.cloned.1.call-done = bf16[16,192]{1,0:T(8,128)(2,1)} async-done(((bf16[128,192]{1,0:T(8,128)(2,1)}), bf16[16,192]{1,0:T(8,128)(2,1)}) %reduce-scatter.9.cloned.1.call-update) | async-done | bytes 6160
  132.0 1.0 multiply_reduce_fusion.1
  133.0 0.2 convolution_convert_fusion.9
  133.2 0.6 reshape.172
  133.8 3.3 %all-to-all-start.2 = ((bf16[8,2,192]{2,1,0:T(2,128)(2,1)}), bf16[8,2,192]{2,1,0:T(2,128)(2,1)S(1)}, u32[]{:S(2)}, u32[]{:S(2)}) async-start(bf16[8,2,192]{2,1,0:T(2,128)(2,1)} %reshape.172), calls=%async_computation.2 | async-start | bytes 16384 | tf_op jit(solution)/shard_map/all_to_all | solution.py:164
  137.2 1.6 fusion.70
  138.8 1.6 fusion.69
  140.4 2.3 all-to-all-done.2
  142.7 0.2 convolution_convert_fusion.8
  142.9 0.1 fusion.67
  143.0 1.1 fusion.68
  144.1 3.2 %fusion.9 = bf16[1536,384]{1,0:T(8,128)(2,1)S(1)} fusion(f32[1536,384]{1,0:T(8,128)} %get-tuple-element.58, f32[12,384]{1,0:T(8,128)S(1)} %fusion.67), kind=kLoop, calls=%fused_computation.14 | loop fusion | flops 11796480 | bytes 3557376 | tf_op jit(solution)/shard_map/convert_element_type | solution.py:179
  147.4 1.2 convolution_bitcast_fusion
  148.6 0.9 fusion.19
  149.5 32.4 %psum.55 = f32[192]{0:T(256)} all-reduce(f32[192]{0:T(256)S(1)} %get-tuple-element.45), channel_id=1, replica_groups=mesh['groups'=2,'geom'=4,'design'=2,'head'=2] {'geom','design','head'}, use_global_device_ids=true, to_apply=%region_19.20 | all-reduce | flops 192 | bytes 1536 | tf_op jit(solution)/shard_map/psum | solution.py:186
  181.9 1.4 fusion.2
  183.3 60.8 %all-reduce.3.cloned.1.call-done = (f32[192,384]{1,0:T(8,128)}, f32[384,192]{0,1:T(8,128)}, f32[192,192]{0,1:T(8,128)}, f32[192,192]{1,0:T(8,128)}, f32[192,192]{1,0:T(8,128)}, /*index=5*/f32[192,192]{1,0:T(8,128)}) async-done(((f32[192,384]{1,0:T(8,128)}, f32[384,192]{0,1:T(8,128)}, f32[192,192]{0,1:T(8,128)}, f32[192,192]{1,0:T(8,128)}, f32[192,192]{1,0:T(8,128)}, /*index=5*/f32[192,192]{1,0:T(8,128)}), ...) | async-done | bytes 1179664 | tf_op jit(solution)/shard_map/psum | solution.py:186
  244.0 1.8 copy.57
  245.8 1.7 copy.74
  247.5 1.7 copy.75
  249.2 1.6 copy.76
  250.8 1.6 copy.77
  252.4 0.7 copy.78
  (40 shorter events, 0.3 us)
Async XLA Ops:
  7.2 8.8 %copy-start = (bf16[1,1536,192]{1,2,0:T(8,128)(2,1)S(1)}, bf16[1,1536,192]{1,2,0:T(8,128)(2,1)}, u32[]{:S(2)}) copy-start(bf16[1,1536,192]{1,2,0:T(8,128)(2,1)} %param.12) | copy-start | bytes 1769476
  9.6 15.0 %all-to-all-start = ((bf16[8,1,2]{2,1,0:T(2,128)(2,1)}), bf16[8,1,2]{2,1,0:T(2,128)(2,1)S(1)}, u32[]{:S(2)}, u32[]{:S(2)}) async-start(bf16[8,1,2]{2,1,0:T(2,128)(2,1)} %convert_element_type.190), calls=%async_computation | async-start | bytes 8192 | tf_op jit(solution)/shard_map/all_to_all | solution.py:82
  16.0 4.0 %copy-start.3 = (bf16[384,192]{0,1:T(8,128)(2,1)S(1)}, bf16[384,192]{0,1:T(8,128)(2,1)}, u32[]{:S(2)}) copy-start(bf16[384,192]{0,1:T(8,128)(2,1)} %param.19) | copy-start | bytes 442372
  20.0 0.9 copy-start.1
  20.6 15.0 %copy-start.11 = (f32[192]{0:T(256)S(1)}, f32[192]{0:T(256)}, u32[]{:S(2)}) copy-start(f32[192]{0:T(256)} %param.17) | copy-start | bytes 2308
  20.9 14.4 %copy-start.12 = (bf16[1,16,192]{2,1,0:T(8,128)(2,1)S(1)}, bf16[1,16,192]{2,1,0:T(8,128)(2,1)}, u32[]{:S(2)}) copy-start(bf16[1,16,192]{2,1,0:T(8,128)(2,1)} %param.14) | copy-start | bytes 18436
  20.9 14.8 %copy-start.6 = (bf16[192,192]{1,0:T(8,128)(2,1)S(1)}, bf16[192,192]{1,0:T(8,128)(2,1)}, u32[]{:S(2)}) copy-start(bf16[192,192]{1,0:T(8,128)(2,1)} %param.21) | copy-start | bytes 221188
  20.9 14.9 %copy-start.5 = (bf16[192,192]{1,0:T(8,128)(2,1)S(1)}, bf16[192,192]{1,0:T(8,128)(2,1)}, u32[]{:S(2)}) copy-start(bf16[192,192]{1,0:T(8,128)(2,1)} %param.22) | copy-start | bytes 221188
  24.6 10.7 %all-to-all-start.1 = ((bf16[8,2,192]{2,1,0:T(2,128)(2,1)}), bf16[8,2,192]{2,1,0:T(2,128)(2,1)S(1)}, u32[]{:S(2)}, u32[]{:S(2)}) async-start(bf16[8,2,192]{2,1,0:T(2,128)(2,1)} %copy.50), calls=%async_computation.1 | async-start | bytes 16384 | tf_op jit(solution)/shard_map/all_to_all | solution.py:75
  29.7 70.8 %reduce-scatter.7.cloned.1.call-start = ((), (), s32[]{:S(2)}) async-start(), calls=%async_computation.5 | async-start | bytes 73728
  69.4 2.3 copy-start.2
  71.7 60.3 %reduce-scatter.9.cloned.1.call-start = ((), (), s32[]{:S(2)}) async-start(), calls=%async_computation.6 | async-start | bytes 73728
  72.6 70.3 %copy-start.4 = (bf16[384,192]{0,1:T(8,128)(2,1)S(1)}, bf16[384,192]{0,1:T(8,128)(2,1)}, u32[]{:S(2)}) copy-start(bf16[384,192]{0,1:T(8,128)(2,1)} %param.19) | copy-start | bytes 442372
  72.6 70.4 %copy-start.10 = (f32[12,384]{1,0:T(8,128)S(1)}, f32[12,384]{1,0:T(8,128)}, u32[]{:S(2)}) copy-start(f32[12,384]{1,0:T(8,128)} %convert_reduce_fusion) | copy-start | bytes 55300
  133.8 8.9 %all-to-all-start.2 = ((bf16[8,2,192]{2,1,0:T(2,128)(2,1)}), bf16[8,2,192]{2,1,0:T(2,128)(2,1)S(1)}, u32[]{:S(2)}, u32[]{:S(2)}) async-start(bf16[8,2,192]{2,1,0:T(2,128)(2,1)} %reshape.172), calls=%async_computation.2 | async-start | bytes 16384 | tf_op jit(solution)/shard_map/all_to_all | solution.py:164
  137.1 106.9 %all-reduce.3.cloned.1.call-start = ((), (), s32[]{:S(2)}) async-start(), calls=%async_computation.7 | async-start | bytes 2752512 | tf_op jit(solution)/shard_map/psum | solution.py:186
  147.3 1.2 copy-start.7
  147.3 34.6 %copy-start.9 = (bf16[192,384]{1,0:T(8,128)(2,1)S(1)}, bf16[192,384]{1,0:T(8,128)(2,1)}, u32[]{:S(2)}) copy-start(bf16[192,384]{1,0:T(8,128)(2,1)} %param.18) | copy-start | bytes 442372
  244.0 8.4 %copy-start.8 = (f32[192,192]{1,0:T(8,128)S(1)}, f32[192,192]{1,0:T(8,128)}, u32[]{:S(2)}) copy-start(f32[192,192]{1,0:T(8,128)} %get-tuple-element.71) | copy-start | bytes 442372
Sparse Core Ops, SparseCore 0:
  71.8 28.6 reduce-scatter.6
  103.3 28.5 reduce-scatter.8
  148.7 95.3 all-reduce.2
where the time goes:
time: 260 us
  waiting for transfers between devices  126 us (48%)
  blocking collectives  60.4 us (23%)
  matrix products  25.1 us (10%)
  starting transfers between devices  14.9 us (6%)
  between operations  14 us (5%)
  local copies, waits for them, and re-layouts  13.3 us (5%)
  other arithmetic  6.46 us (2%)
    psum x1, waiting for transfers between devices, on_device(): lax.psum((grad_in, grad_out, grad_query, grad_key, grad_value, grad_proj,...  60.8 us
    unnamed x5, waiting for transfers between devices  57.2 us
    psum x1, blocking collectives, on_device(): lax.psum((grad_in, grad_out, grad_query, grad_key, grad_value, grad_proj,...  32.4 us
    all_gather x1, blocking collectives, on_device(): lax.all_gather(key_local, ('geom', 'head'), axis=0, tiled=True)  14 us
    all_gather x1, blocking collectives, on_device(): lax.all_gather(value_local, ('geom', 'head'), axis=0, tiled=True)  14 us
    unnamed x34, local copies, waits for them, and re-layouts  10.7 us
    dot_general x8, matrix products, contract_rows(): lax.dot_general(first_arg, second_arg, (((0,), (0,)), ((), ())), precisio...  7.61 us
    all_to_all x1, starting transfers between devices, on_device(): lax.all_to_all(slot_anchor.astype(jnp.float32).reshape(owners, CAP).astyp...  6.35 us
  transfers between devices with their start and end apart: 6, of which 5 were waited for; matrix products, arithmetic and copies ran while one was open for 7% of the time, Pallas kernels for 0%

commit v1 on v0

--- a/solution.py
+++ b/solution.py
@@ -184,8 +184,11 @@
     grad_in = contract_rows(points, d_pre)
     d_input = times_transposed(d_pre, w_in).astype(jnp.bfloat16)
     reduced = lax.psum(
-        (grad_in, grad_out, grad_query, grad_key, grad_value, grad_proj, grad_gain),
-        ("geom", "design", "head"),
+        lax.psum(
+            (grad_in, grad_out, grad_query, grad_key, grad_value, grad_proj, grad_gain),
+            ("design", "head"),
+        ),
+        "geom",
     )
     return (
         attended[None],

time: 260 us -> 270 us (1.038)
  waiting for transfers between devices: 126 us -> 149 us
  blocking collectives: 60.4 us -> 46.8 us
    psum x0 -> x1, waiting for transfers between devices: none -> 44.7 us  [on_device(): lax.psum(lax.psum((grad_in, grad_out, grad_query, grad_key, grad_value, g...]
    psum x1, blocking collectives: 32.4 us -> 5.73 us  [on_device(): lax.psum((grad_in, grad_out, grad_query, grad_key, grad_value, grad_proj,...]
    psum x1, waiting for transfers between devices: 60.8 us -> 39.4 us  [on_device(): lax.psum((grad_in, grad_out, grad_query, grad_key, grad_value, grad_proj,...]
    psum x0 -> x1, blocking collectives: none -> 13.1 us  [on_device(): lax.psum(lax.psum((grad_in, grad_out, grad_query, grad_key, grad_value, g...]
    unnamed x5 -> x6, waiting for transfers between devices: 57.2 us -> 57.2 us
  transfers between devices with their start and end apart: 6 -> 7, of which waited for: 5 -> 6; matrix products, arithmetic and copies ran while one was open for 7% -> 6% of each run, Pallas kernels for 0% -> 0%
where the time goes in v1:
time: 270 us; the launch traced here: 269 us
  waiting for transfers between devices  149 us (55%)
  blocking collectives  46.8 us (17%)
  matrix products  25.1 us (9%)
  starting transfers between devices  14.9 us (6%)
  between operations  14 us (5%)
  local copies, waits for them, and re-layouts  13.3 us (5%)
  other arithmetic  6.46 us (2%)
    unnamed x6, waiting for transfers between devices  57.2 us
    psum x1, waiting for transfers between devices, on_device(): lax.psum(lax.psum((grad_in, grad_out, grad_query, grad_key, grad_value, g...  44.7 us
    psum x1, waiting for transfers between devices, on_device(): lax.psum((grad_in, grad_out, grad_query, grad_key, grad_value, grad_proj,...  39.4 us
    all_gather x1, blocking collectives, on_device(): lax.all_gather(key_local, ('geom', 'head'), axis=0, tiled=True)  14 us
    all_gather x1, blocking collectives, on_device(): lax.all_gather(value_local, ('geom', 'head'), axis=0, tiled=True)  14 us
    psum x1, blocking collectives, on_device(): lax.psum(lax.psum((grad_in, grad_out, grad_query, grad_key, grad_value, g...  13.1 us
    unnamed x34, local copies, waits for them, and re-layouts  10.7 us
    dot_general x8, matrix products, contract_rows(): lax.dot_general(first_arg, second_arg, (((0,), (0,)), ((), ())), precisio...  7.61 us
  transfers between devices with their start and end apart: 7, of which 6 were waited for; matrix products, arithmetic and copies ran while one was open for 6% of the time, Pallas kernels for 0%

profile of v1, /device:TPU:0, one launch (start us, length us, event | category | flops | bytes accessed | tf_op | source)
XLA Modules:
  0.0 269.4 jit_solution(9408385870738555010)
XLA Ops:
  7.2 0.7 and_select_fusion
  7.9 0.7 add_bitcast_fusion
  8.6 0.2 convert_reduce_fusion.2
  8.8 0.1 select_reduce_fusion
  8.9 0.7 convert_element_type.190
  9.6 6.4 %all-to-all-start = ((bf16[8,1,2]{2,1,0:T(2,128)(2,1)}), bf16[8,1,2]{2,1,0:T(2,128)(2,1)S(1)}, u32[]{:S(2)}, u32[]{:S(2)}) async-start(bf16[8,1,2]{2,1,0:T(2,128)(2,1)} %convert_element_type.190), calls=%async_computation | async-start | bytes 8192 | tf_op jit(solution)/shard_map/all_to_all | solution.py:82
  16.0 3.2 %multiply_convert_fusion = (bf16[1536,384]{1,0:T(8,128)(2,1)S(1)}, f32[1536,384]{1,0:T(8,128)}) fusion(bf16[192,384]{1,0:T(8,128)(2,1)} %param.18, bf16[1,1536,192]{1,2,0:T(8,128)(2,1)S(1)} %copy-done), kind=kOutput, calls=%fused_computation.19 | convolution fusion | flops 231800832 | bytes 4276224 | tf_op jit(solution)/shard_map/dot_general | solution.py:69
  19.2 0.8 convert_reduce_fusion
  20.0 0.6 fusion.64
  20.6 0.2 reshape.166
  20.8 0.1 copy-done.1
  20.9 1.2 convolution_convert_fusion.5
  22.1 1.2 convolution_convert_fusion.1
  23.3 0.5 reduce_sum.95
  23.8 0.2 convolution_convert_fusion.12
  23.9 0.7 copy.50
  24.6 5.1 %all-to-all-start.1 = ((bf16[8,2,192]{2,1,0:T(2,128)(2,1)}), bf16[8,2,192]{2,1,0:T(2,128)(2,1)S(1)}, u32[]{:S(2)}, u32[]{:S(2)}) async-start(bf16[8,2,192]{2,1,0:T(2,128)(2,1)} %copy.50), calls=%async_computation.1 | async-start | bytes 16384 | tf_op jit(solution)/shard_map/all_to_all | solution.py:75
  29.8 0.1 convert_element_type.158
  29.9 0.1 convert_reduce_fusion.1
  30.0 5.3 %all-to-all-done.1 = bf16[8,2,192]{2,1,0:T(2,128)(2,1)S(1)} async-done(((bf16[8,2,192]{2,1,0:T(2,128)(2,1)}), bf16[8,2,192]{2,1,0:T(2,128)(2,1)S(1)}, u32[]{:S(2)}, u32[]{:S(2)}) %all-to-all-start.1) | async-done | bytes 6176 | tf_op jit(solution)/shard_map/all_to_all | solution.py:75
  35.4 0.2 multiply_reduce_fusion.3
  35.7 0.1 convolution_convert_fusion.10
  35.8 0.1 convolution_convert_fusion.11
  36.0 14.0 %all_gather.6 = bf16[128,192]{1,0:T(8,128)(2,1)S(1)} all-gather(bf16[16,192]{1,0:T(8,128)(2,1)S(1)} %convolution_convert_fusion.11), channel_id=1, replica_groups=mesh['groups'=2,'geom'=4,'design'=2,'head'=2] {'geom','head'}, dimensions={0}, use_global_device_ids=true | all-gather | bytes 55296 | tf_op jit(solution)/shard_map/all_gather | solution.py:102
  50.0 0.1 copy.51
  50.1 14.0 %all_gather.7 = bf16[128,192]{1,0:T(8,128)(2,1)S(1)} all-gather(bf16[16,192]{1,0:T(8,128)(2,1)S(1)} %convolution_convert_fusion.10), channel_id=1, replica_groups=mesh['groups'=2,'geom'=4,'design'=2,'head'=2] {'geom','head'}, dimensions={0}, use_global_device_ids=true | all-gather | bytes 55296 | tf_op jit(solution)/shard_map/all_gather | solution.py:101
  64.1 0.1 copy.52
  64.2 0.3 fusion.65
  64.5 1.3 fusion.63
  65.8 1.8 convolution_convert_fusion.7
  67.6 1.8 convolution_convert_fusion.2
  69.4 0.6 convolution_convert_fusion.4
  70.0 0.9 convolution_bitcast_fusion.1
  70.9 0.7 copy.64
  71.7 0.9 fusion.30
  72.6 0.6 convolution_convert_fusion.6
  73.2 0.7 copy.66
  74.0 26.5 %reduce-scatter.7.cloned.1.call-done = bf16[16,192]{1,0:T(8,128)(2,1)} async-done(((bf16[128,192]{1,0:T(8,128)(2,1)}), bf16[16,192]{1,0:T(8,128)(2,1)}) %reduce-scatter.7.cloned.1.call-update) | async-done | bytes 6160
  100.5 0.8 fusion.66
  101.4 30.6 %reduce-scatter.9.cloned.1.call-done = bf16[16,192]{1,0:T(8,128)(2,1)} async-done(((bf16[128,192]{1,0:T(8,128)(2,1)}), bf16[16,192]{1,0:T(8,128)(2,1)}) %reduce-scatter.9.cloned.1.call-update) | async-done | bytes 6160
  132.0 1.0 multiply_reduce_fusion.1
  133.0 0.2 convolution_convert_fusion.9
  133.2 0.6 reshape.172
  133.8 3.3 %all-to-all-start.2 = ((bf16[8,2,192]{2,1,0:T(2,128)(2,1)}), bf16[8,2,192]{2,1,0:T(2,128)(2,1)S(1)}, u32[]{:S(2)}, u32[]{:S(2)}) async-start(bf16[8,2,192]{2,1,0:T(2,128)(2,1)} %reshape.172), calls=%async_computation.2 | async-start | bytes 16384 | tf_op jit(solution)/shard_map/all_to_all | solution.py:164
  137.2 1.6 fusion.70
  138.8 1.6 fusion.69
  140.4 2.3 all-to-all-done.2
  142.7 0.2 convolution_convert_fusion.8
  142.9 0.1 fusion.67
  143.0 1.1 fusion.68
  144.1 3.2 %fusion.9 = bf16[1536,384]{1,0:T(8,128)(2,1)S(1)} fusion(f32[1536,384]{1,0:T(8,128)} %get-tuple-element.64, f32[12,384]{1,0:T(8,128)S(1)} %fusion.67), kind=kLoop, calls=%fused_computation.14 | loop fusion | flops 11796480 | bytes 3557376 | tf_op jit(solution)/shard_map/convert_element_type | solution.py:179
  147.4 1.2 convolution_bitcast_fusion
  148.6 39.4 %all-reduce.5.cloned.1.call-done = (f32[192,384]{1,0:T(8,128)}, f32[384,192]{0,1:T(8,128)}, f32[192,192]{0,1:T(8,128)}, f32[192,192]{1,0:T(8,128)}, f32[192,192]{1,0:T(8,128)}, /*index=5*/f32[192,192]{1,0:T(8,128)}) async-done(((f32[192,384]{1,0:T(8,128)}, f32[384,192]{0,1:T(8,128)}, f32[192,192]{0,1:T(8,128)}, f32[192,192]{1,0:T(8,128)}, f32[192,192]{1,0:T(8,128)}, /*index=5*/f32[192,192]{1,0:T(8,128)}), ...) | async-done | bytes 1179664 | tf_op jit(solution)/shard_map/psum | solution.py:187
  188.1 0.9 fusion.19
  189.0 5.7 %psum.110 = f32[192]{0:T(256)S(1)} all-reduce(f32[192]{0:T(256)S(1)} %get-tuple-element.45), channel_id=1, replica_groups=mesh['groups'=2,'geom'=4,'design'=2,'head'=2] {'design','head'}, use_global_device_ids=true, to_apply=%region_25.26 | all-reduce | flops 192 | bytes 1536 | tf_op jit(solution)/shard_map/psum | solution.py:187
  194.7 13.1 %psum.111 = f32[192]{0:T(256)} all-reduce(f32[192]{0:T(256)S(1)} %psum.110), channel_id=1, replica_groups=mesh['groups'=2,'geom'=4,'design'=2,'head'=2] {'geom'}, use_global_device_ids=true, to_apply=%region_26.27 | all-reduce | flops 192 | bytes 1536 | tf_op jit(solution)/shard_map/psum | solution.py:186
  207.8 1.4 fusion.2
  209.2 44.7 %all-reduce.7.cloned.1.call-done = (f32[192,384]{1,0:T(8,128)}, f32[384,192]{0,1:T(8,128)}, f32[192,192]{0,1:T(8,128)}, f32[192,192]{1,0:T(8,128)}, f32[192,192]{1,0:T(8,128)}, /*index=5*/f32[192,192]{1,0:T(8,128)}) async-done(((f32[192,384]{1,0:T(8,128)}, f32[384,192]{0,1:T(8,128)}, f32[192,192]{0,1:T(8,128)}, f32[192,192]{1,0:T(8,128)}, f32[192,192]{1,0:T(8,128)}, /*index=5*/f32[192,192]{1,0:T(8,128)}), ...) | async-done | bytes 1179664 | tf_op jit(solution)/shard_map/psum | solution.py:186
  253.8 1.8 copy.57
  255.6 1.7 copy.80
  257.3 1.7 copy.81
  259.0 1.6 copy.82
  260.6 1.6 copy.83
  262.2 0.7 copy.84
  (44 shorter events, 0.5 us)
Async XLA Ops:
  7.2 8.8 %copy-start = (bf16[1,1536,192]{1,2,0:T(8,128)(2,1)S(1)}, bf16[1,1536,192]{1,2,0:T(8,128)(2,1)}, u32[]{:S(2)}) copy-start(bf16[1,1536,192]{1,2,0:T(8,128)(2,1)} %param.12) | copy-start | bytes 1769476
  9.6 15.0 %all-to-all-start = ((bf16[8,1,2]{2,1,0:T(2,128)(2,1)}), bf16[8,1,2]{2,1,0:T(2,128)(2,1)S(1)}, u32[]{:S(2)}, u32[]{:S(2)}) async-start(bf16[8,1,2]{2,1,0:T(2,128)(2,1)} %convert_element_type.190), calls=%async_computation | async-start | bytes 8192 | tf_op jit(solution)/shard_map/all_to_all | solution.py:82
  16.0 4.0 %copy-start.3 = (bf16[384,192]{0,1:T(8,128)(2,1)S(1)}, bf16[384,192]{0,1:T(8,128)(2,1)}, u32[]{:S(2)}) copy-start(bf16[384,192]{0,1:T(8,128)(2,1)} %param.19) | copy-start | bytes 442372
  20.0 0.9 copy-start.1
  20.6 15.0 %copy-start.11 = (f32[192]{0:T(256)S(1)}, f32[192]{0:T(256)}, u32[]{:S(2)}) copy-start(f32[192]{0:T(256)} %param.17) | copy-start | bytes 2308
  20.9 14.4 %copy-start.12 = (bf16[1,16,192]{2,1,0:T(8,128)(2,1)S(1)}, bf16[1,16,192]{2,1,0:T(8,128)(2,1)}, u32[]{:S(2)}) copy-start(bf16[1,16,192]{2,1,0:T(8,128)(2,1)} %param.14) | copy-start | bytes 18436
  20.9 14.8 %copy-start.6 = (bf16[192,192]{1,0:T(8,128)(2,1)S(1)}, bf16[192,192]{1,0:T(8,128)(2,1)}, u32[]{:S(2)}) copy-start(bf16[192,192]{1,0:T(8,128)(2,1)} %param.21) | copy-start | bytes 221188
  20.9 14.9 %copy-start.5 = (bf16[192,192]{1,0:T(8,128)(2,1)S(1)}, bf16[192,192]{1,0:T(8,128)(2,1)}, u32[]{:S(2)}) copy-start(bf16[192,192]{1,0:T(8,128)(2,1)} %param.22) | copy-start | bytes 221188
  24.6 10.7 %all-to-all-start.1 = ((bf16[8,2,192]{2,1,0:T(2,128)(2,1)}), bf16[8,2,192]{2,1,0:T(2,128)(2,1)S(1)}, u32[]{:S(2)}, u32[]{:S(2)}) async-start(bf16[8,2,192]{2,1,0:T(2,128)(2,1)} %copy.50), calls=%async_computation.1 | async-start | bytes 16384 | tf_op jit(solution)/shard_map/all_to_all | solution.py:75
  29.7 70.8 %reduce-scatter.7.cloned.1.call-start = ((), (), s32[]{:S(2)}) async-start(), calls=%async_computation.5 | async-start | bytes 73728
  69.4 2.3 copy-start.2
  71.7 60.3 %reduce-scatter.9.cloned.1.call-start = ((), (), s32[]{:S(2)}) async-start(), calls=%async_computation.6 | async-start | bytes 73728
  72.6 70.3 %copy-start.4 = (bf16[384,192]{0,1:T(8,128)(2,1)S(1)}, bf16[384,192]{0,1:T(8,128)(2,1)}, u32[]{:S(2)}) copy-start(bf16[384,192]{0,1:T(8,128)(2,1)} %param.19) | copy-start | bytes 442372
  72.6 70.4 %copy-start.10 = (f32[12,384]{1,0:T(8,128)S(1)}, f32[12,384]{1,0:T(8,128)}, u32[]{:S(2)}) copy-start(f32[12,384]{1,0:T(8,128)} %convert_reduce_fusion) | copy-start | bytes 55300
  133.8 8.9 %all-to-all-start.2 = ((bf16[8,2,192]{2,1,0:T(2,128)(2,1)}), bf16[8,2,192]{2,1,0:T(2,128)(2,1)S(1)}, u32[]{:S(2)}, u32[]{:S(2)}) async-start(bf16[8,2,192]{2,1,0:T(2,128)(2,1)} %reshape.172), calls=%async_computation.2 | async-start | bytes 16384 | tf_op jit(solution)/shard_map/all_to_all | solution.py:164
  137.1 50.9 %all-reduce.5.cloned.1.call-start = ((), (), s32[]{:S(2)}) async-start(), calls=%async_computation.7 | async-start | bytes 2752512 | tf_op jit(solution)/shard_map/psum | solution.py:187
  147.3 40.7 %copy-start.7 = (bf16[192,192]{1,0:T(8,128)(2,1)S(1)}, bf16[192,192]{1,0:T(8,128)(2,1)}, u32[]{:S(2)}) copy-start(bf16[192,192]{1,0:T(8,128)(2,1)} %param.23) | copy-start | bytes 221188
  147.3 60.4 %copy-start.9 = (bf16[192,384]{1,0:T(8,128)(2,1)S(1)}, bf16[192,384]{1,0:T(8,128)(2,1)}, u32[]{:S(2)}) copy-start(bf16[192,384]{1,0:T(8,128)(2,1)} %param.18) | copy-start | bytes 442372
  148.6 105.3 %all-reduce.7.cloned.1.call-start = ((), (), s32[]{:S(2)}) async-start(), calls=%async_computation.8 | async-start | bytes 2752512 | tf_op jit(solution)/shard_map/psum | solution.py:186
  253.8 8.4 %copy-start.8 = (f32[192,192]{1,0:T(8,128)S(1)}, f32[192,192]{1,0:T(8,128)}, u32[]{:S(2)}) copy-start(f32[192,192]{1,0:T(8,128)} %get-tuple-element.77) | copy-start | bytes 442372
Sparse Core Ops, SparseCore 0:
  71.8 28.6 reduce-scatter.6
  103.3 28.5 reduce-scatter.8
  148.7 39.2 all-reduce.4
  190.7 63.0 all-reduce.6
